TPU v7x, 256 devices: a 4x2x16 block of a 4x16x16 slice. The times are simulated.
256 devices in a mesh: groups: 2 (over y), gx: 32 (over z, core), gy: 4 (over x).
Axes of the slice: x: 4, y: 2, z: 16, core: 2. Of those that a mesh axis runs over, the one named last changes fastest.
The devices are a block of a 4x16x16 slice.
Arguments:
- initial_state: float32 [64, 4, 65536], P(('groups', 'gx'), 'gy'), parts along dimension 0, may hold values from -80 to 80
- fields: float32 [46], P('groups'), parts along dimension 0, may hold values from -3 to 3
- bond_order: int32 [4, 6], replicated, may hold values from 0 to 5, each once within a row
Outputs:
- amplitudes: float32 [64, 4, 65536], P(('groups', 'gx'), 'gy'), parts along dimension 0
There are 2 independent parts, one for each index of `groups`. A program takes and returns all parts, laid end to end along the dimension named above; an argument that names none is the same for every part. Nothing has to cross between parts.
Inputs may be any that keep to these rules, and one draw needn't show every extreme that they name: `bond_order`: each row is an ordering of the six bonds of its window; entry e names the bond between sites s_w + e and s_w + e + 1.
All inputs are finite; a program needn't handle non-finite values.
Results may differ from a plain program's by a relative error of at most 0.0001.
Values sent between devices are 32-bit elements; how exact they have to be, the bound alone decides.
A program may use at most 64 MiB of HBM per device.

v0:
```python
import jax
import jax.numpy as jnp
from jax import lax
from jax.sharding import Mesh
from jax.sharding import PartitionSpec as P

GX_GY = ("gx_0", "gx_1", "gy")
GX = ("gx_0", "gx_1")
GROUPS_GX = ("groups", "gx_0", "gx_1")


coupling = 1.0
step_time = 0.15
epsilon = 1e-06
HIGHEST = lax.Precision.HIGHEST


def cut_along(shard, dim, devices):
    shape = shard.shape
    parts = shard.reshape(*shape[:dim], devices, shape[dim] // devices, *shape[dim + 1 :])
    return jnp.moveaxis(parts, dim, 0)


def laid_out(parts, dim):
    parts = jnp.moveaxis(parts, 0, dim)
    shape = parts.shape
    return parts.reshape(*shape[:dim], shape[dim] * shape[dim + 1], *shape[dim + 2 :])


def one_exchange(shard, axis, axes, splits, concats):
    sizes = [lax.axis_size(a) for a in axes]
    parts = cut_along(shard, splits[0], sizes[0])
    parts = jnp.moveaxis(cut_along(parts, splits[1] + 1, sizes[1]), 0, 1)
    inside = parts.shape[2:]
    parts = parts.reshape(-1, *inside)
    parts = lax.all_to_all(parts, axis, split_axis=0, concat_axis=0, tiled=True)
    parts = laid_out(parts.reshape(*sizes, *inside), concats[0] + 1)
    return laid_out(parts, concats[1])


def one_axis_at_a_time(shard, axes):
    for axis in axes:
        shard = lax.psum(shard, axis)
    return shard


def make_gates(fields):
    left_field = fields[:-1]
    right_field = fields[1:]
    half_sum = 0.5 * (left_field + right_field)
    half_diff = 0.5 * (left_field - right_field)
    radius = jnp.sqrt(half_diff * half_diff + 4.0 * coupling * coupling)
    boosted = jnp.exp(step_time * coupling) * jnp.ones_like(half_sum)
    cosine = jnp.cosh(step_time * radius)
    sine_ratio = jnp.sinh(step_time * radius) / radius
    corner_low = jnp.exp(-step_time * (coupling + half_sum))
    corner_high = jnp.exp(-step_time * (coupling - half_sum))
    middle_up = boosted * (cosine - sine_ratio * half_diff)
    middle_down = boosted * (cosine + sine_ratio * half_diff)
    flipping = -2.0 * coupling * boosted * sine_ratio
    nothing = jnp.zeros_like(half_sum)
    entries = [
        corner_low,
        nothing,
        nothing,
        nothing,
        nothing,
        middle_up,
        flipping,
        nothing,
        nothing,
        flipping,
        middle_down,
        nothing,
        nothing,
        nothing,
        nothing,
        corner_high,
    ]
    return jnp.stack(entries, axis=1).reshape(-1, 4, 4)


def pair_apply(matrix, gate, first_bit, second_bit, count_bits):
    tensor = gate.reshape(2, 2, 2, 2)
    shaped = matrix.reshape((2,) * count_bits + (matrix.shape[1],))
    axis_first = count_bits - 1 - first_bit
    axis_second = count_bits - 1 - second_bit
    moved = jnp.tensordot(
        tensor, shaped, axes=([2, 3], [axis_first, axis_second]), precision=HIGHEST
    )
    return jnp.moveaxis(moved, [0, 1], [axis_first, axis_second]).reshape(matrix.shape)


def window_start(position, local_bits):
    return (0, 7, local_bits - 7, 1)[position % 4]


def window_matrix(bond_gates, order_row, start_bit):
    identity = jnp.eye(128, dtype=jnp.float32)
    singles = [
        pair_apply(identity, bond_gates[start_bit + offset], offset, offset + 1, 7)
        for offset in range(6)
    ]
    matrix = identity
    for section_number in range(6):
        chosen = jnp.zeros_like(identity)
        for offset in range(6):
            chosen = (
                chosen + (order_row[section_number] == offset).astype(jnp.float32) * singles[offset]
            )
        matrix = jnp.dot(chosen, matrix, precision=HIGHEST)
    return matrix


def apply_window(vector, matrix, start_bit):
    if start_bit == 0:
        shaped = vector.reshape(-1, 128)
        return jnp.dot(shaped, matrix.T, precision=HIGHEST).reshape(-1)
    if start_bit == 1:
        widened = jnp.kron(matrix, jnp.eye(2, dtype=jnp.float32))
        shaped = vector.reshape(-1, 256)
        return jnp.dot(shaped, widened.T, precision=HIGHEST).reshape(-1)
    shaped = vector.reshape(-1, 128, 2**start_bit)
    return jnp.einsum("hg,agb->ahb", matrix, shaped, precision=HIGHEST).reshape(-1)


def evolve_windows(vector, bond_gates, bond_order, local_bits):

    def one_cycle(cycle_number, current):
        for position in range(4):
            start_bit = window_start(position, local_bits)
            order_row = lax.dynamic_index_in_dim(
                bond_order, 4 * cycle_number + position, 0, keepdims=False
            )
            current = apply_window(
                current, window_matrix(bond_gates, order_row, start_bit), start_bit
            )
        return current

    return lax.fori_loop(0, bond_order.shape[0] // 4, one_cycle, vector)


def device_matrix(bond_gates, local_bits, count_bits):
    matrix = jnp.eye(2**count_bits, dtype=jnp.float32)
    matrix = pair_apply(matrix, bond_gates[local_bits - 1], count_bits - 1, 0, count_bits)
    for offset in range(count_bits - 2):
        matrix = pair_apply(matrix, bond_gates[local_bits + offset], offset, offset + 1, count_bits)
    return matrix


def regroup_out(vector, across_x, across_y):
    shaped = vector.reshape(2, across_x, across_y, -1)
    return one_exchange(shaped, GX_GY, (GX, "gy"), (1, 2), (1, 2)).reshape(-1)


def regroup_back(vector, across_x, across_y):
    shaped = vector.reshape(2, across_x, across_y, -1)
    return lax.all_to_all(
        lax.all_to_all(shaped, "gy", split_axis=2, concat_axis=2, tiled=True),
        GX,
        split_axis=1,
        concat_axis=1,
        tiled=True,
    ).reshape(-1)


def total_squares(vector):
    return one_axis_at_a_time(jnp.sum(vector * vector), GX_GY)


def local(initial_state, fields, bond_order):
    amps_device = initial_state.shape[2]
    local_bits = amps_device.bit_length() - 1
    across_x = lax.axis_size(GX)
    across_y = lax.axis_size("gy")
    xbits_count = across_x.bit_length() - 1
    ybits_count = across_y.bit_length() - 1
    bond_gates = make_gates(fields)
    vector = evolve_windows(initial_state.reshape(-1), bond_gates, bond_order, local_bits)
    joined = device_matrix(bond_gates, local_bits, 1 + xbits_count + ybits_count)
    regrouped = regroup_out(vector, across_x, across_y)
    mixed = jnp.dot(joined, regrouped.reshape(joined.shape[0], -1), precision=HIGHEST).reshape(-1)
    summed = total_squares(mixed)
    restored = regroup_back(mixed, across_x, across_y)
    count_all = float(amps_device * across_x * across_y)
    scaled = restored * lax.rsqrt(summed / count_all + epsilon)
    return scaled.reshape(initial_state.shape)


def solution(mesh):
    torus = Mesh(
        mesh.devices.reshape(mesh.shape["groups"], 16, 2, mesh.shape["gy"]),
        ("groups", "gx_0", "gx_1", "gy"),
    )
    placed = (P(GROUPS_GX, "gy", None), P("groups"), P())
    return jax.shard_map(
        local, mesh=torus, in_specs=placed, out_specs=P(GROUPS_GX, "gy", None), check_vma=False
    )
```

profile of v0, /device:TPU:33, one launch (start us, length us, event | category | flops | bytes accessed | tf_op | source)
XLA Modules:
  0.0 256.7 jit_solution(14003122860373444206)
XLA Ops:
  0.0 2.1 fusion.52
  24.4 1.5 fusion.53
  48.4 0.8 multiply_bitcast_fusion
  50.3 0.4 convolution_bitcast_fusion.24
  50.6 0.3 convolution_bitcast_fusion.19
  51.3 0.3 convolution_bitcast_fusion.20
  51.7 0.3 convolution_bitcast_fusion.27
  74.5 0.4 convolution_bitcast_fusion.30
  75.3 0.3 convolution_bitcast_fusion.31
  75.6 0.3 convolution_bitcast_fusion.13
  76.0 0.3 convolution_bitcast_fusion.32
  76.4 0.3 convolution_bitcast_fusion.14
  99.5 0.3 convolution_bitcast_fusion.26
  99.9 0.3 convolution_bitcast_fusion.29
  100.3 0.5 bitcast_add_fusion.80
  101.9 0.3 convolution_bitcast_fusion.33
  102.3 0.3 convolution_bitcast_fusion.35
  103.1 0.5 bitcast_add_fusion.110
  106.8 0.4 convolution_bitcast_fusion.3
  107.1 0.4 convolution_bitcast_fusion.2
  107.8 0.3 convolution_bitcast_fusion.18
  108.2 0.4 convolution_bitcast_fusion.17
  108.7 0.5 bitcast_add_fusion.50
  109.2 0.4 bitcast_add_fusion.30
  111.4 0.6 convolution_bitcast_fusion.1
  112.4 0.4 convolution_bitcast_fusion.11
  112.9 0.5 bitcast_add_fusion.20
  115.4 6.6 %broadcast_multiply_fusion = f32[128,2,128,2]{3,2,1,0:T(8,128)} fusion(f32[2,2]{1,0:T(2,128)S(1)} %compare_convert_fusion, f32[128,128]{1,0:T(8,128)S(1)} %fusion.76), kind=kLoop, calls=%fused_computation | loop fusion | flops 65536 | bytes 327696 | tf_op jit(solution)/shard_map/while/body/eval_jaxpr/jit(kron)/mul | solution.py:120
  122.0 12.7 %reshape.1797 = f32[256,256,1,1]{1,0,2,3:T(8,128)S(1)} reshape(f32[128,2,128,2]{3,2,1,0:T(8,128)} %broadcast_multiply_fusion) | data formatting | bytes 524288 | tf_op jit(solution)/shard_map/while/body/eval_jaxpr/jit(kron)/mul | solution.py:120
  134.7 0.4 convolution_bitcast_fusion
  135.1 0.9 copy.1026
  136.1 31.0 %all-to-all-start = ((f32[128,2,1,1,256]{4,1,3,2,0:T(2,128)}), f32[128,2,1,1,256]{4,1,3,2,0:T(2,128)S(1)}, u32[]{:S(2)}, u32[]{:S(2)}) async-start(f32[128,2,1,1,256]{4,1,3,2,0:T(2,128)} %bitcast.478), calls=%async_computation | async-start | bytes 524288 | tf_op jit(solution)/shard_map/all_to_all | solution.py:36
  168.4 0.9 convolution_bitcast_fusion.10
  169.3 1.2 convolution_bitcast_fusion.9
  170.5 1.2 convolution_bitcast_fusion.8
  171.8 1.2 convolution_bitcast_fusion.7
  173.0 1.2 convolution_bitcast_fusion.6
  174.2 1.2 convolution_bitcast_fusion.5
  175.4 1.2 convolution_bitcast_fusion.4
  177.0 12.8 %all-to-all-done = f32[128,2,1,1,256]{4,1,3,2,0:T(2,128)S(1)} async-done(((f32[128,2,1,1,256]{4,1,3,2,0:T(2,128)}), f32[128,2,1,1,256]{4,1,3,2,0:T(2,128)S(1)}, u32[]{:S(2)}, u32[]{:S(2)}) %all-to-all-start) | async-done | bytes 262176 | tf_op jit(solution)/shard_map/all_to_all | solution.py:36
  190.0 1.1 multiply_reduce_fusion
  191.2 8.7 %all_to_all.15 = f32[2,32,4,256]{3,1,0,2:T(8,128)S(1)} all-to-all(f32[2,32,4,256]{3,1,0,2:T(8,128)S(1)} %copy.1029), channel_id=1, replica_groups=mesh['groups'=2,'gx_0'=16,'gx_1'=2,'gy'=4] {'gy'}, dimensions={2} | all-to-all | bytes 524288 | tf_op jit(solution)/shard_map/all_to_all | solution.py:159
  199.9 0.9 copy.1030
  200.7 5.1 %all-to-all-start.2 = ((f32[2,32,4,256]{3,2,0,1:T(4,128)}), f32[2,32,4,256]{3,2,0,1:T(4,128)S(1)}, u32[]{:S(2)}, u32[]{:S(2)}) async-start(f32[2,32,4,256]{3,2,0,1:T(4,128)} %copy.1030), calls=%async_computation.2 | async-start | bytes 524288 | tf_op jit(solution)/shard_map/all_to_all | solution.py:158
  205.9 32.2 %psum.21 = f32[]{:T(128)} all-reduce(f32[]{:T(128)} %get-tuple-element.105), channel_id=1, replica_groups=mesh['groups'=2,'gx_0'=16,'gx_1'=2,'gy'=4] {'gx_0'}, use_global_device_ids=true, to_apply=%region_1.2 | all-reduce | flops 1 | bytes 8 | tf_op jit(solution)/shard_map/psum | solution.py:43
  238.0 9.3 %psum.22 = f32[]{:T(128)} all-reduce(f32[]{:T(128)} %psum.21), channel_id=1, replica_groups=mesh['groups'=2,'gx_0'=16,'gx_1'=2,'gy'=4] {'gx_1'}, use_global_device_ids=true, to_apply=%region_2.3 | all-reduce | flops 1 | bytes 8 | tf_op jit(solution)/shard_map/psum | solution.py:43
  247.3 7.5 %psum.23 = f32[]{:T(128)} all-reduce(f32[]{:T(128)} %psum.22), channel_id=1, replica_groups=mesh['groups'=2,'gx_0'=16,'gx_1'=2,'gy'=4] {'gy'}, use_global_device_ids=true, to_apply=%region_3.4 | all-reduce | flops 1 | bytes 8 | tf_op jit(solution)/shard_map/psum | solution.py:43
  255.7 1.0 mul.2403
  (117 shorter events, 13.4 us)
Async XLA Ops:
  0.0 106.8 %copy-start = (f32[1,1,65536]{2,1,0:T(1,128)S(1)}, f32[1,1,65536]{2,1,0:T(1,128)}, u32[]{:S(2)}) copy-start(f32[1,1,65536]{2,1,0:T(1,128)} %param.3) | copy-start | bytes 786436
  136.1 53.7 %all-to-all-start = ((f32[128,2,1,1,256]{4,1,3,2,0:T(2,128)}), f32[128,2,1,1,256]{4,1,3,2,0:T(2,128)S(1)}, u32[]{:S(2)}, u32[]{:S(2)}) async-start(f32[128,2,1,1,256]{4,1,3,2,0:T(2,128)} %bitcast.478), calls=%async_computation | async-start | bytes 524288 | tf_op jit(solution)/shard_map/all_to_all | solution.py:36
  200.7 54.6 %all-to-all-start.2 = ((f32[2,32,4,256]{3,2,0,1:T(4,128)}), f32[2,32,4,256]{3,2,0,1:T(4,128)S(1)}, u32[]{:S(2)}, u32[]{:S(2)}) async-start(f32[2,32,4,256]{3,2,0,1:T(4,128)} %copy.1030), calls=%async_computation.2 | async-start | bytes 524288 | tf_op jit(solution)/shard_map/all_to_all | solution.py:158
where the time goes:
time: 259 us; the launch traced here: 257 us
  between operations  91.6 us (35%)
  blocking collectives  57.6 us (22%)
  starting transfers between devices  36.1 us (14%)
  local copies, waits for them, and re-layouts  24.8 us (10%)
  matrix products  24.3 us (9%)
  waiting for transfers between devices  12.8 us (5%)
  other arithmetic  9.47 us (4%)
    psum x3, blocking collectives, one_axis_at_a_time(): shard = lax.psum(shard, axis)  48.9 us
    all_to_all x1, starting transfers between devices, one_exchange(): parts = lax.all_to_all(parts, axis, split_axis=0, concat_axis=0, tiled=True)  31 us
    dot_general x31, matrix products, pair_apply(): jnp.tensordot(tensor, shaped, axes=([2, 3], [axis_first, axis_second]), p...  16.7 us
    all_to_all x1, waiting for transfers between devices, one_exchange(): parts = lax.all_to_all(parts, axis, split_axis=0, concat_axis=0, tiled=True)  12.8 us
    mul x1, local copies, waits for them, and re-layouts, apply_window(): widened = jnp.kron(matrix, jnp.eye(2, dtype=jnp.float32))  12.7 us
    all_to_all x1, blocking collectives, regroup_back(): lax.all_to_all(shaped, 'gy', split_axis=2, concat_axis=2, tiled=True)  8.69 us
    mul x1, other arithmetic, apply_window(): widened = jnp.kron(matrix, jnp.eye(2, dtype=jnp.float32))  6.58 us
  transfers between devices with their start and end apart: 2, of which 1 were waited for; matrix products, arithmetic and copies ran while one was open for 4% of the time, Pallas kernels for 0%

commit v1 on v0

v1 whole, which is shorter than its diff:
```python
import functools

import jax
import jax.numpy as jnp
from jax import lax
from jax.experimental import pallas as pl
from jax.experimental.pallas import tpu as pltpu
from jax.sharding import PartitionSpec as P

MESH = pl.DeviceIdType.MESH
STEP = 0.15
BOOST = 1.161834242728283
EPSILON = 1e-06
STARTS = (0, 7, 9, 1)


def gate_entries(left, right, shape):
    left = jnp.full(shape, left, jnp.float32)
    right = jnp.full(shape, right, jnp.float32)
    half_sum = 0.5 * (left + right)
    half_diff = 0.5 * (left - right)
    radius = jnp.sqrt(half_diff * half_diff + 4.0)
    grow = jnp.exp(STEP * radius)
    decay = jnp.exp(-STEP * radius)
    cosine = 0.5 * (grow + decay)
    sine_ratio = 0.5 * (grow - decay) / radius
    low = jnp.exp(-STEP * (1.0 + half_sum))
    high = jnp.exp(-STEP * (1.0 - half_sum))
    up = BOOST * (cosine - sine_ratio * half_diff)
    down = BOOST * (cosine + sine_ratio * half_diff)
    flip = -2.0 * BOOST * sine_ratio
    return low, up, down, high, flip


def bond_step(matrix, fields, start, offset, lane):
    low, up, down, high, flip = gate_entries(
        fields[start + offset], fields[start + offset + 1], lane.shape
    )
    first = (lane >> offset) & 1
    second = (lane >> (offset + 1)) & 1
    zero = first == 0
    equal = first == second
    diagonal = jnp.where(equal, jnp.where(zero, low, high), jnp.where(zero, up, down))
    from_below = jnp.where(equal, 0.0, jnp.where(zero, flip, 0.0))
    from_above = jnp.where(equal, 0.0, jnp.where(zero, 0.0, flip))
    shift = jnp.left_shift(1, offset)
    return (
        matrix * diagonal
        + pltpu.roll(matrix, shift, 1) * from_below
        + pltpu.roll(matrix, 128 - shift, 1) * from_above
    )


def split(x):
    high = x.astype(jnp.bfloat16)
    return high, (x - high.astype(jnp.float32)).astype(jnp.bfloat16)


def dot(a, b):
    return jnp.dot(a, b, preferred_element_type=jnp.float32)


def dot_split(a, b):
    return dot(a[0], b[0]) + (dot(a[0], b[1]) + dot(a[1], b[0]))


def mix(value, entries, bit):
    low, up, down, high, flip = entries
    rows = value.shape[0]
    inner = 2**bit
    v = value.reshape(rows // (4 * inner), 2, 2, inner // 8, 8, 128)
    both0, only_first = v[:, 0, 0], v[:, 0, 1]
    only_second, both1 = v[:, 1, 0], v[:, 1, 1]
    new = jnp.stack(
        [
            jnp.stack([low * both0, down * only_first + flip * only_second], axis=1),
            jnp.stack([up * only_second + flip * only_first, high * both1], axis=1),
        ],
        axis=1,
    )
    return new.reshape(value.shape)


def kernel(
    x_ref,
    fields,
    order,
    o_ref,
    t_ref,
    send,
    held,
    back,
    final,
    part_z,
    part_xc,
    got_z,
    got_xc,
    send_sems,
    recv_sems,
    got_z_sem,
    got_xc_sem,
):
    gx, gy = lax.axis_index("gx"), lax.axis_index("gy")
    n_z, n_x = lax.axis_size("gx") // 2, lax.axis_size("gy")
    n = 2 * n_z * n_x
    z, core = gx // 2, gx % 2
    me = gx * n_x + gy

    def partner(k):
        t, u = k // (2 * n_x), (k + 1) % (2 * n_x)
        dz = n_z // 2 + ((t + 1) // 2) * (2 * (t % 2) - 1)
        tz = (z + dz + n_z) % n_z
        tc, tx = (core + u % 2) % 2, (gy + u // 2) % n_x
        return 2 * tz + tc, tx

    barrier = pltpu.get_barrier_semaphore()

    @pl.loop(0, n - 1)
    def _(k):
        px, py = partner(k)
        pl.semaphore_signal(barrier, inc=1, device_id={"gx": px, "gy": py}, device_id_type=MESH)

    lane = lax.broadcasted_iota(jnp.int32, (1, 128), 1)
    row = lax.broadcasted_iota(jnp.int32, (128, 128), 0)
    col = lax.broadcasted_iota(jnp.int32, (128, 128), 1)
    identity = jnp.where(row == col, 1.0, 0.0)
    mats = [identity] * 4
    for e in range(6):
        for w in range(4):
            at = e if w in (0, 3) else 5 - e
            mats[w] = bond_step(mats[w], fields, STARTS[w], order[6 * w + at], lane)
    w0t, w1, w2, w3t = [split(m) for m in mats]
    i0 = lax.broadcasted_iota(jnp.int32, (256, 128), 0)
    g0 = lax.broadcasted_iota(jnp.int32, (256, 128), 1)
    g1 = lax.broadcasted_iota(jnp.int32, (128, 256), 0)
    j1 = lax.broadcasted_iota(jnp.int32, (128, 256), 1)
    left = jnp.where((i0 >> 1) == g0, 1.0, 0.0).astype(jnp.bfloat16)
    right = jnp.where((j1 >> 1) == g1, 1.0, 0.0).astype(jnp.bfloat16)
    ii = lax.broadcasted_iota(jnp.int32, (256, 256), 0)
    jj = lax.broadcasted_iota(jnp.int32, (256, 256), 1)
    same = ((ii ^ jj) & 1) == 0
    w3k = [
        jnp.where(same, dot(dot(left, m).astype(jnp.bfloat16), right), 0.0).astype(jnp.bfloat16)
        for m in w3t
    ]

    for b in range(4):
        rows = slice(128 * b, 128 * (b + 1))
        y = dot_split(split(x_ref[rows, :]), w0t)
        t_ref[rows, :] = dot_split(w1, split(y))
    for n8 in range(2):
        ys = []
        for n7 in range(2):
            t = t_ref[pl.ds(n7 + 2 * n8, 128, stride=4), :]
            ys.append(dot_split(w2, split(t)))
        out = dot_split(split(jnp.concatenate(ys, axis=1)), w3k)
        for n15 in range(2):
            for n7 in range(2):
                send[pl.ds(4 * n8 + 2 * n15 + n7, 64, stride=8), :] = out[
                    64 * n15 : 64 * (n15 + 1), 128 * n7 : 128 * (n7 + 1)
                ]

    pl.semaphore_wait(barrier, n - 1)

    def exchange(source, target, which):
        source, target = source.reshape(n, 4, 128), target.reshape(n, 4, 128)

        @pl.loop(0, n - 1)
        def _(k):
            px, py = partner(k)
            pltpu.make_async_remote_copy(
                src_ref=source.at[px * n_x + py],
                dst_ref=target.at[me],
                send_sem=send_sems.at[which],
                recv_sem=recv_sems.at[which],
                device_id={"gx": px, "gy": py},
                device_id_type=MESH,
            ).start()

        target[me] = source[me]

    def arrived(source, target, which):
        part = pl.ds(0, 4 * (n - 1))
        copy = pltpu.make_async_copy(source.at[part], target.at[part], recv_sems.at[which])
        copy.wait()

    def sent(source, target, which):
        part = pl.ds(0, 4 * (n - 1))
        copy = pltpu.make_async_copy(source.at[part], target.at[part], send_sems.at[which])
        copy.wait()

    exchange(send, held, 0)
    entries = [
        gate_entries(fields[15 + k], fields[16 + k], (1, 128)) for k in range(7)
    ]
    srow = lax.broadcasted_iota(jnp.int32, (8, 128), 0)
    bit1, bit2 = (srow >> 1) & 1, (srow >> 2) & 1
    low, up, down, high, flip = entries[0]
    d15 = jnp.where(bit1 == bit2, jnp.where(bit1 == 0, low, high), jnp.where(bit1 == 0, up, down))
    f15 = jnp.where(bit1 == bit2, 0.0, flip)
    below15 = jnp.where(bit1 == 0, f15, 0.0)
    above15 = jnp.where(bit1 == 0, 0.0, f15)
    low, up, down, high, flip = entries[1]
    d16_0 = jnp.where(bit2 == 0, low, down)
    f16_0 = jnp.where(bit2 == 0, 0.0, flip)
    d16_1 = jnp.where(bit2 == 0, up, high)
    f16_1 = jnp.where(bit2 == 0, flip, 0.0)
    arrived(send, held, 0)

    for c in range(n // 8):
        v = held[32 * c : 32 * (c + 1), :].reshape(4, 8, 128)
        v = v * d15 + pltpu.roll(v, 2, 1) * below15 + pltpu.roll(v, 6, 1) * above15
        v = v.reshape(2, 2, 8, 128)
        v0, v1 = v[:, 0], v[:, 1]
        u0 = v0 * d16_0 + pltpu.roll(v1, 4, 1) * f16_0
        u1 = v1 * d16_1 + pltpu.roll(v0, 4, 1) * f16_1
        v = jnp.stack([u0, u1], axis=1).reshape(32, 128)
        t_ref[32 * c : 32 * (c + 1), :] = mix(v, entries[2], 3)
    total = jnp.zeros((8, 128), jnp.float32)
    for h in range(2):
        v = jnp.concatenate(
            [t_ref[16 * g + 8 * h : 16 * g + 8 * h + 8, :] for g in range(4 * n // 16)], axis=0
        )
        for k in range(4):
            v = mix(v, entries[3 + k], 3 + k)
        total = total + jnp.sum((v * v).reshape(-1, 8, 128), axis=0)
        for g in range(4 * n // 16):
            back[16 * g + 8 * h : 16 * g + 8 * h + 8, :] = v[8 * g : 8 * (g + 1)]

    part_z[...] = jnp.sum(total, axis=0, keepdims=True)

    def small(source, target, slot, px, py, s_sem, r_sem):
        return pltpu.make_async_remote_copy(
            src_ref=source,
            dst_ref=target.at[slot],
            send_sem=s_sem,
            recv_sem=r_sem,
            device_id={"gx": px, "gy": py},
            device_id_type=MESH,
        )

    @pl.loop(1, n_z)
    def _(k):
        tz = (z + k) % n_z
        small(part_z, got_z, z, 2 * tz + core, gy, send_sems.at[2], got_z_sem.at[0]).start()

    got_z[z] = part_z[...]
    exchange(back, final, 1)
    mine = core * n_x + gy
    pltpu.make_async_copy(
        got_z.at[pl.ds(0, n_z - 1)], got_z.at[pl.ds(0, n_z - 1)], got_z_sem.at[0]
    ).wait()
    part_xc[...] = jnp.sum(got_z[...], axis=0)

    @pl.loop(1, 2 * n_x)
    def _(k):
        tc, tx = (core + k % 2) % 2, (gy + k // 2) % n_x
        small(part_xc, got_xc, mine, 2 * z + tc, tx, send_sems.at[3], got_xc_sem.at[0]).start()

    got_xc[mine] = part_xc[...]
    pltpu.make_async_copy(
        got_xc.at[pl.ds(0, 2 * n_x - 1)], got_xc.at[pl.ds(0, 2 * n_x - 1)], got_xc_sem.at[0]
    ).wait()
    summed = jnp.sum(jnp.sum(got_xc[...], axis=0), axis=1, keepdims=True)
    count = float(x_ref.shape[0] * x_ref.shape[1] * n)
    scale = lax.rsqrt(summed / count + EPSILON)
    arrived(back, final, 1)
    for n15 in range(2):
        for n7 in range(2):
            o_ref[pl.ds(n15 * 256 + n7, 128, stride=2), :] = (
                final[pl.ds(2 * n15 + n7, 128, stride=4), :] * scale
            )
    sent(send, held, 0)
    sent(back, final, 1)
    pltpu.make_async_copy(
        got_z.at[pl.ds(0, n_z - 1)], got_z.at[pl.ds(0, n_z - 1)], send_sems.at[2]
    ).wait()
    pltpu.make_async_copy(
        got_xc.at[pl.ds(0, 2 * n_x - 1)], got_xc.at[pl.ds(0, 2 * n_x - 1)], send_sems.at[3]
    ).wait()


def local(initial_state, fields, bond_order):
    amps = initial_state.shape[2]
    n = lax.axis_size("gx") * lax.axis_size("gy")
    n_z, n_xc = lax.axis_size("gx") // 2, 2 * lax.axis_size("gy")
    block = pltpu.VMEM((amps // 128, 128), jnp.float32)
    vmem, smem = pl.BlockSpec(memory_space=pltpu.VMEM), pl.BlockSpec(memory_space=pltpu.SMEM)
    out = pl.pallas_call(
        kernel,
        out_shape=jax.ShapeDtypeStruct((amps // 128, 128), jnp.float32),
        in_specs=[vmem, smem, smem],
        out_specs=vmem,
        scratch_shapes=[
            block,
            block,
            block,
            block,
            block,
            pltpu.VMEM((1, 128), jnp.float32),
            pltpu.VMEM((1, 128), jnp.float32),
            pltpu.VMEM((n_z, 1, 128), jnp.float32),
            pltpu.VMEM((n_xc, 1, 128), jnp.float32),
            pltpu.SemaphoreType.DMA((4,)),
            pltpu.SemaphoreType.DMA((2,)),
            pltpu.SemaphoreType.DMA((1,)),
            pltpu.SemaphoreType.DMA((1,)),
        ],
        compiler_params=pltpu.CompilerParams(collective_id=0, has_side_effects=True),
    )(initial_state.reshape(amps // 128, 128), fields, bond_order.reshape(-1))
    return out.reshape(initial_state.shape)


def solution(mesh):
    placed = (P(("groups", "gx"), "gy", None), P("groups"), P())
    return jax.shard_map(
        local,
        mesh=mesh,
        in_specs=placed,
        out_specs=P(("groups", "gx"), "gy", None),
        check_vma=False,
    )
```

time: 259 us -> 69 us (0.27)
  between operations: 91.6 us -> 0.01 us
  Pallas kernels: 0 us -> 65.8 us
  blocking collectives: 57.6 us -> 0 us
  starting transfers between devices: 36.1 us -> 0 us
  matrix products: 24.3 us -> 0 us
  local copies, waits for them, and re-layouts: 24.8 us -> 2.94 us
  waiting for transfers between devices: 12.8 us -> 0 us
  other arithmetic: 9.47 us -> 0 us
    pallas_call x0 -> x1, Pallas kernels: none -> 65.8 us  [local(): pl.pallas_call(kernel, out_shape=jax.ShapeDtypeStruct((amps // 128, 128),...]
    psum x3 -> x0, blocking collectives: 48.9 us -> none  [one_axis_at_a_time(): shard = lax.psum(shard, axis)]
    all_to_all x2 -> x0, starting transfers between devices: 36.1 us -> none  [the longest x1 31 us: one_exchange(): parts = lax.all_to_all(parts, axis, split_axis=0, concat_axis=0, tiled=True)]
    dot_general x60 -> x0, matrix products: 24.3 us -> none  [the longest x31 16.7 us: pair_apply(): jnp.tensordot(tensor, shaped, axes=([2, 3], [axis_first, axis_second]), p...]
    mul x3 -> x0, local copies, waits for them, and re-layouts: 13.9 us -> none  [the longest x1 12.7 us: apply_window(): widened = jnp.kron(matrix, jnp.eye(2, dtype=jnp.float32))]
    all_to_all x2 -> x0, waiting for transfers between devices: 12.8 us -> none  [the longest x1 12.8 us: one_exchange(): parts = lax.all_to_all(parts, axis, split_axis=0, concat_axis=0, tiled=True)]
    all_to_all x1 -> x0, blocking collectives: 8.69 us -> none  [regroup_back(): lax.all_to_all(shaped, 'gy', split_axis=2, concat_axis=2, tiled=True)]
    mul x2 -> x0, other arithmetic: 6.67 us -> none  [the longest x1 6.58 us: apply_window(): widened = jnp.kron(matrix, jnp.eye(2, dtype=jnp.float32))]
  transfers between devices with their start and end apart: 2 -> 0, of which waited for: 1 -> 0; matrix products, arithmetic and copies ran while one was open for 4% -> 0% of each run, Pallas kernels for 0% -> 0%
where the time goes in v1:
time: 69 us; the launch traced here: 68.8 us
  Pallas kernels  65.8 us (95%)
  local copies, waits for them, and re-layouts  2.94 us (4%)
    pallas_call x1, Pallas kernels, local(): pl.pallas_call(kernel, out_shape=jax.ShapeDtypeStruct((amps // 128, 128),...  65.8 us
    unnamed x1, local copies, waits for them, and re-layouts  1.67 us

profile of v1, /device:TPU:33, one launch (start us, length us, event | category | flops | bytes accessed | tf_op | source)
XLA Modules:
  0.0 68.8 jit_solution(1092727139279052732)
XLA Ops:
  0.0 1.3 %reshape.10.order = s32[24]{0:T(128)} reshape(s32[4,6]{1,0:T(4,128)} %param.5) | data formatting | bytes 192 | tf_op jit(solution)/shard_map/reshape | solution.py:310
  1.3 65.8 %shard_map.37 = f32[512,128]{1,0:T(8,128)} custom-call(f32[512,128]{1,0:T(8,128)} %bitcast.3, f32[23]{0:T(128)} %fields.1, s32[24]{0:T(128)} %reshape.10.order), custom_call_target="tpu_custom_call" | custom-call | tf_op jit(solution)/shard_map/pallas_call | solution.py:289
  67.1 1.7 %copy.5 = f32[1,1,65536]{2,1,0:T(1,128)} copy(f32[1,1,65536]{2,1,0:T(1,128)} %bitcast.2) | data formatting | bytes 524288

commit v2 on v1

--- a/solution.py
+++ b/solution.py
@@ -82,10 +82,11 @@
 
 
 def kernel(
-    x_ref,
+    x_hbm,
     fields,
     order,
     o_ref,
+    x_ref,
     t_ref,
     send,
     held,
@@ -99,26 +100,85 @@
     recv_sems,
     got_z_sem,
     got_xc_sem,
+    fetch_sem,
+    ready,
 ):
     gx, gy = lax.axis_index("gx"), lax.axis_index("gy")
     n_z, n_x = lax.axis_size("gx") // 2, lax.axis_size("gy")
-    n = 2 * n_z * n_x
+    plane = 2 * n_x
+    n = n_z * plane
     z, core = gx // 2, gx % 2
-    me = gx * n_x + gy
-
-    def partner(k):
-        t, u = k // (2 * n_x), (k + 1) % (2 * n_x)
+    mine = core * n_x + gy
+    me = z * plane + mine
+
+    fetch = pltpu.make_async_copy(x_hbm, x_ref, fetch_sem)
+    fetch.start()
+
+    def at(tz, i):
+        return {"gx": 2 * tz + i // n_x, "gy": i % n_x}
+
+    def far_first(t):
         dz = n_z // 2 + ((t + 1) // 2) * (2 * (t % 2) - 1)
-        tz = (z + dz + n_z) % n_z
-        tc, tx = (core + u % 2) % 2, (gy + u // 2) % n_x
-        return 2 * tz + tc, tx
+        return (z + dz + n_z) % n_z
 
     barrier = pltpu.get_barrier_semaphore()
 
-    @pl.loop(0, n - 1)
-    def _(k):
-        px, py = partner(k)
-        pl.semaphore_signal(barrier, inc=1, device_id={"gx": px, "gy": py}, device_id_type=MESH)
+    @pl.when(me > 0)
+    def _():
+        for i in range(plane):
+
+            @pl.when(mine < i)
+            def _():
+                pl.semaphore_signal(barrier, inc=1, device_id=at(z, i), device_id_type=MESH)
+
+        @pl.loop(z + 1, n_z)
+        def _(tz):
+            for i in range(plane):
+                pl.semaphore_signal(barrier, inc=1, device_id=at(tz, i), device_id_type=MESH)
+
+        pl.semaphore_signal(barrier, inc=1, device_id=at(0, 0), device_id_type=MESH)
+
+    @pl.when(me != 1)
+    def _():
+        pl.semaphore_wait(barrier, (me + n - 1) % n)
+
+    @pl.when(me > 0)
+    def _():
+        @pl.loop(0, z)
+        def _(tz):
+            for i in range(plane):
+
+                def answer():
+                    pl.semaphore_signal(
+                        ready.at[z], inc=1, device_id=at(tz, i), device_id_type=MESH
+                    )
+
+                if i == 0:
+                    pl.when(tz > 0)(answer)
+                else:
+                    answer()
+
+        for i in range(plane):
+
+            @pl.when((i < mine) & (z * plane + i > 0))
+            def _():
+                pl.semaphore_signal(ready.at[z], inc=1, device_id=at(z, i), device_id_type=MESH)
+
+    @pl.when(me == 0)
+    def _():
+        @pl.loop(0, n_z)
+        def _(tz):
+            for i in range(plane):
+
+                def answer():
+                    pl.semaphore_signal(
+                        ready.at[n_z], inc=1, device_id=at(tz, i), device_id_type=MESH
+                    )
+
+                if i == 0:
+                    pl.when(tz > 0)(answer)
+                else:
+                    answer()
 
     lane = lax.broadcasted_iota(jnp.int32, (1, 128), 1)
     row = lax.broadcasted_iota(jnp.int32, (128, 128), 0)
@@ -127,8 +187,8 @@
     mats = [identity] * 4
     for e in range(6):
         for w in range(4):
-            at = e if w in (0, 3) else 5 - e
-            mats[w] = bond_step(mats[w], fields, STARTS[w], order[6 * w + at], lane)
+            step = e if w in (0, 3) else 5 - e
+            mats[w] = bond_step(mats[w], fields, STARTS[w], order[w, step], lane)
     w0t, w1, w2, w3t = [split(m) for m in mats]
     i0 = lax.broadcasted_iota(jnp.int32, (256, 128), 0)
     g0 = lax.broadcasted_iota(jnp.int32, (256, 128), 1)
@@ -144,6 +204,7 @@
         for m in w3t
     ]
 
+    fetch.wait()
     for b in range(4):
         rows = slice(128 * b, 128 * (b + 1))
         y = dot_split(split(x_ref[rows, :]), w0t)
@@ -160,24 +221,27 @@
                     64 * n15 : 64 * (n15 + 1), 128 * n7 : 128 * (n7 + 1)
                 ]
 
-    pl.semaphore_wait(barrier, n - 1)
-
-    def exchange(source, target, which):
+    def post(source, target, which, tz, i):
         source, target = source.reshape(n, 4, 128), target.reshape(n, 4, 128)
-
-        @pl.loop(0, n - 1)
-        def _(k):
-            px, py = partner(k)
-            pltpu.make_async_remote_copy(
-                src_ref=source.at[px * n_x + py],
-                dst_ref=target.at[me],
-                send_sem=send_sems.at[which],
-                recv_sem=recv_sems.at[which],
-                device_id={"gx": px, "gy": py},
-                device_id_type=MESH,
-            ).start()
-
+        pltpu.make_async_remote_copy(
+            src_ref=source.at[tz * plane + i],
+            dst_ref=target.at[me],
+            send_sem=send_sems.at[which],
+            recv_sem=recv_sems.at[which],
+            device_id=at(tz, i),
+            device_id_type=MESH,
+        ).start()
+
+    def keep(source, target):
+        source, target = source.reshape(n, 4, 128), target.reshape(n, 4, 128)
         target[me] = source[me]
+
+    def post_known(tz):
+        for i in range(plane):
+            if i == 0:
+                pl.when(tz > 0)(functools.partial(post, send, held, 0, tz, i))
+            else:
+                post(send, held, 0, tz, i)
 
     def arrived(source, target, which):
         part = pl.ds(0, 4 * (n - 1))
@@ -189,7 +253,35 @@
         copy = pltpu.make_async_copy(source.at[part], target.at[part], send_sems.at[which])
         copy.wait()
 
-    exchange(send, held, 0)
+    @pl.loop(0, n_z - 1)
+    def _(t):
+        tz = far_first(t)
+
+        @pl.when((tz < z) | (me == 0))
+        def _():
+            post_known(tz)
+
+    @pl.when((me > 0) & (mine < plane - 1))
+    def _():
+        pl.semaphore_wait(ready.at[z], plane - 1 - mine)
+
+    for i in range(plane):
+
+        @pl.when((i != mine) & (z * plane + i > 0))
+        def _():
+            post(send, held, 0, z, i)
+
+    @pl.when(me > 0)
+    def _():
+        @pl.loop(z + 1, n_z)
+        def _(tz):
+            pl.semaphore_wait(ready.at[tz], plane)
+            post_known(tz)
+
+        pl.semaphore_wait(ready.at[n_z], 1)
+        post(send, held, 0, 0, 0)
+
+    keep(send, held)
     entries = [
         gate_entries(fields[15 + k], fields[16 + k], (1, 128)) for k in range(7)
     ]
@@ -245,8 +337,20 @@
         small(part_z, got_z, z, 2 * tz + core, gy, send_sems.at[2], got_z_sem.at[0]).start()
 
     got_z[z] = part_z[...]
-    exchange(back, final, 1)
-    mine = core * n_x + gy
+
+    @pl.loop(0, n_z - 1)
+    def _(t):
+        tz = far_first(t)
+        for i in range(plane):
+            post(back, final, 1, tz, i)
+
+    for i in range(plane):
+
+        @pl.when(i != mine)
+        def _():
+            post(back, final, 1, z, i)
+
+    keep(back, final)
     pltpu.make_async_copy(
         got_z.at[pl.ds(0, n_z - 1)], got_z.at[pl.ds(0, n_z - 1)], got_z_sem.at[0]
     ).wait()
@@ -289,9 +393,10 @@
     out = pl.pallas_call(
         kernel,
         out_shape=jax.ShapeDtypeStruct((amps // 128, 128), jnp.float32),
-        in_specs=[vmem, smem, smem],
+        in_specs=[pl.BlockSpec(memory_space=pl.ANY), smem, smem],
         out_specs=vmem,
         scratch_shapes=[
+            block,
             block,
             block,
             block,
@@ -305,9 +410,11 @@
             pltpu.SemaphoreType.DMA((2,)),
             pltpu.SemaphoreType.DMA((1,)),
             pltpu.SemaphoreType.DMA((1,)),
+            pltpu.SemaphoreType.DMA,
+            pltpu.SemaphoreType.REGULAR((n_z + 1,)),
         ],
         compiler_params=pltpu.CompilerParams(collective_id=0, has_side_effects=True),
-    )(initial_state.reshape(amps // 128, 128), fields, bond_order.reshape(-1))
+    )(initial_state.reshape(amps // 128, 128), fields, bond_order)
     return out.reshape(initial_state.shape)
 
 

time: 69 us -> 62.5 us (0.906)
  Pallas kernels: 65.8 us -> 60.7 us
  local copies, waits for them, and re-layouts: 2.94 us -> 1.67 us
    pallas_call x1, Pallas kernels: 65.8 us -> 60.7 us  [local(): pl.pallas_call(kernel, out_shape=jax.ShapeDtypeStruct((amps // 128, 128),...]
    reshape x1 -> x0, local copies, waits for them, and re-layouts: 1.27 us -> none  [local(): bond_order.reshape(-1)]
where the time goes in v2:
time: 62.5 us; the launch traced here: 62.4 us
  Pallas kernels  60.7 us (97%)
  local copies, waits for them, and re-layouts  1.67 us (3%)
    pallas_call x1, Pallas kernels, local(): pl.pallas_call(kernel, out_shape=jax.ShapeDtypeStruct((amps // 128, 128),...  60.7 us
    unnamed x1, local copies, waits for them, and re-layouts  1.67 us

profile of v2, /device:TPU:33, one launch (start us, length us, event | category | flops | bytes accessed | tf_op | source)
XLA Modules:
  0.0 62.4 jit_solution(16669964839686325685)
XLA Ops:
  0.0 60.7 %shard_map.37 = f32[512,128]{1,0:T(8,128)} custom-call(f32[512,128]{1,0:T(8,128)} %bitcast.3, f32[23]{0:T(128)} %fields.1, s32[4,6]{1,0:T(4,128)} %order.1), custom_call_target="tpu_custom_call" | custom-call | tf_op jit(solution)/shard_map/pallas_call | solution.py:393
  60.7 1.7 %copy.5 = f32[1,1,65536]{2,1,0:T(1,128)} copy(f32[1,1,65536]{2,1,0:T(1,128)} %bitcast.2) | data formatting | bytes 524288

commit v3 on v2

--- a/solution.py
+++ b/solution.py
@@ -83,9 +83,11 @@
 
 def kernel(
     x_hbm,
+    fields_hbm,
+    order_hbm,
+    o_ref,
     fields,
     order,
-    o_ref,
     x_ref,
     t_ref,
     send,
@@ -100,7 +102,7 @@
     recv_sems,
     got_z_sem,
     got_xc_sem,
-    fetch_sem,
+    fetch_sems,
     ready,
 ):
     gx, gy = lax.axis_index("gx"), lax.axis_index("gy")
@@ -111,7 +113,11 @@
     mine = core * n_x + gy
     me = z * plane + mine
 
-    fetch = pltpu.make_async_copy(x_hbm, x_ref, fetch_sem)
+    fetch = pltpu.make_async_copy(x_hbm, x_ref, fetch_sems.at[0])
+    fetch_fields = pltpu.make_async_copy(fields_hbm, fields, fetch_sems.at[1])
+    fetch_order = pltpu.make_async_copy(order_hbm, order, fetch_sems.at[2])
+    fetch_fields.start()
+    fetch_order.start()
     fetch.start()
 
     def at(tz, i):
@@ -123,66 +129,22 @@
 
     barrier = pltpu.get_barrier_semaphore()
 
+    def greet(device):
+        pl.semaphore_signal(barrier, inc=1, device_id=device, device_id_type=MESH)
+
     @pl.when(me > 0)
     def _():
         for i in range(plane):
 
-            @pl.when(mine < i)
+            @pl.when((mine != i) & (z * plane + i > 0))
             def _():
-                pl.semaphore_signal(barrier, inc=1, device_id=at(z, i), device_id_type=MESH)
-
-        @pl.loop(z + 1, n_z)
-        def _(tz):
-            for i in range(plane):
-                pl.semaphore_signal(barrier, inc=1, device_id=at(tz, i), device_id_type=MESH)
-
-        pl.semaphore_signal(barrier, inc=1, device_id=at(0, 0), device_id_type=MESH)
-
-    @pl.when(me != 1)
-    def _():
-        pl.semaphore_wait(barrier, (me + n - 1) % n)
-
-    @pl.when(me > 0)
-    def _():
-        @pl.loop(0, z)
-        def _(tz):
-            for i in range(plane):
-
-                def answer():
-                    pl.semaphore_signal(
-                        ready.at[z], inc=1, device_id=at(tz, i), device_id_type=MESH
-                    )
-
-                if i == 0:
-                    pl.when(tz > 0)(answer)
-                else:
-                    answer()
-
-        for i in range(plane):
-
-            @pl.when((i < mine) & (z * plane + i > 0))
-            def _():
-                pl.semaphore_signal(ready.at[z], inc=1, device_id=at(z, i), device_id_type=MESH)
-
-    @pl.when(me == 0)
-    def _():
-        @pl.loop(0, n_z)
-        def _(tz):
-            for i in range(plane):
-
-                def answer():
-                    pl.semaphore_signal(
-                        ready.at[n_z], inc=1, device_id=at(tz, i), device_id_type=MESH
-                    )
-
-                if i == 0:
-                    pl.when(tz > 0)(answer)
-                else:
-                    answer()
+                greet(at(z, i))
 
     lane = lax.broadcasted_iota(jnp.int32, (1, 128), 1)
     row = lax.broadcasted_iota(jnp.int32, (128, 128), 0)
     col = lax.broadcasted_iota(jnp.int32, (128, 128), 1)
+    fetch_fields.wait()
+    fetch_order.wait()
     identity = jnp.where(row == col, 1.0, 0.0)
     mats = [identity] * 4
     for e in range(6):
@@ -204,6 +166,33 @@
         for m in w3t
     ]
 
+    @pl.when(me > 0)
+    def _():
+        whole = jnp.where(z > 0, plane - 1, plane - 2)
+        pl.semaphore_wait(barrier, whole + z)
+
+        @pl.loop(0, z)
+        def _(tz):
+            @pl.when(tz * plane + mine > 0)
+            def _():
+                pl.semaphore_signal(
+                    ready.at[z], inc=1, device_id=at(tz, mine), device_id_type=MESH
+                )
+
+        @pl.loop(z + 1, n_z)
+        def _(tz):
+            greet(at(tz, mine))
+
+        @pl.when(mine == 1)
+        def _():
+            greet(at(0, 0))
+
+            @pl.when(z == 0)
+            def _():
+                @pl.loop(1, n_z)
+                def _(tz):
+                    greet(at(tz, 0))
+
     fetch.wait()
     for b in range(4):
         rows = slice(128 * b, 128 * (b + 1))
@@ -253,6 +242,21 @@
         copy = pltpu.make_async_copy(source.at[part], target.at[part], send_sems.at[which])
         copy.wait()
 
+    @pl.when(me == 0)
+    def _():
+        pl.semaphore_wait(barrier, n_z)
+
+        @pl.loop(0, n_z)
+        def _(t):
+            tz = far_first(t)
+            for i in range(plane):
+
+                @pl.when(tz * plane + i > 0)
+                def _():
+                    pl.semaphore_signal(
+                        ready.at[n_z], inc=1, device_id=at(tz, i), device_id_type=MESH
+                    )
+
     @pl.loop(0, n_z - 1)
     def _(t):
         tz = far_first(t)
@@ -260,10 +264,6 @@
         @pl.when((tz < z) | (me == 0))
         def _():
             post_known(tz)
-
-    @pl.when((me > 0) & (mine < plane - 1))
-    def _():
-        pl.semaphore_wait(ready.at[z], plane - 1 - mine)
 
     for i in range(plane):
 
@@ -275,7 +275,7 @@
     def _():
         @pl.loop(z + 1, n_z)
         def _(tz):
-            pl.semaphore_wait(ready.at[tz], plane)
+            pl.semaphore_wait(ready.at[tz], 1)
             post_known(tz)
 
         pl.semaphore_wait(ready.at[n_z], 1)
@@ -389,13 +389,16 @@
     n = lax.axis_size("gx") * lax.axis_size("gy")
     n_z, n_xc = lax.axis_size("gx") // 2, 2 * lax.axis_size("gy")
     block = pltpu.VMEM((amps // 128, 128), jnp.float32)
-    vmem, smem = pl.BlockSpec(memory_space=pltpu.VMEM), pl.BlockSpec(memory_space=pltpu.SMEM)
+    vmem, hbm = pl.BlockSpec(memory_space=pltpu.VMEM), pl.BlockSpec(memory_space=pltpu.HBM)
+    pin = functools.partial(pltpu.with_memory_space_constraint, memory_space=pltpu.HBM)
     out = pl.pallas_call(
         kernel,
         out_shape=jax.ShapeDtypeStruct((amps // 128, 128), jnp.float32),
-        in_specs=[pl.BlockSpec(memory_space=pl.ANY), smem, smem],
+        in_specs=[hbm, hbm, hbm],
         out_specs=vmem,
         scratch_shapes=[
+            pltpu.SMEM(fields.shape, jnp.float32),
+            pltpu.SMEM(bond_order.shape, jnp.int32),
             block,
             block,
             block,
@@ -410,11 +413,15 @@
             pltpu.SemaphoreType.DMA((2,)),
             pltpu.SemaphoreType.DMA((1,)),
             pltpu.SemaphoreType.DMA((1,)),
-            pltpu.SemaphoreType.DMA,
+            pltpu.SemaphoreType.DMA((3,)),
             pltpu.SemaphoreType.REGULAR((n_z + 1,)),
         ],
-        compiler_params=pltpu.CompilerParams(collective_id=0, has_side_effects=True),
-    )(initial_state.reshape(amps // 128, 128), fields, bond_order)
+        compiler_params=pltpu.CompilerParams(
+            collective_id=0, has_side_effects=True, vmem_limit_bytes=4 * 2**20
+        ),
+    )(
+        pin(initial_state.reshape(amps // 128, 128)), pin(fields), pin(bond_order)
+    )
     return out.reshape(initial_state.shape)
 
 

time: 62.5 us -> 58.4 us (0.934)
  Pallas kernels: 60.7 us -> 57.6 us
  local copies, waits for them, and re-layouts: 1.67 us -> 0.71 us
    pallas_call x1, Pallas kernels: 60.7 us -> 57.6 us  [local(): pl.pallas_call(kernel, out_shape=jax.ShapeDtypeStruct((amps // 128, 128),...]
    unnamed x1, local copies, waits for them, and re-layouts: 1.67 us -> 0.71 us
where the time goes in v3:
time: 58.4 us; the launch traced here: 58.3 us
  Pallas kernels  57.6 us (99%)
  local copies, waits for them, and re-layouts  0.71 us (1%)
    pallas_call x1, Pallas kernels, local(): pl.pallas_call(kernel, out_shape=jax.ShapeDtypeStruct((amps // 128, 128),...  57.6 us

profile of v3, /device:TPU:33, one launch (start us, length us, event | category | flops | bytes accessed | tf_op | source)
XLA Modules:
  0.0 58.3 jit_solution(13220945595203374550)
XLA Ops:
  0.0 57.6 %shard_map.37 = f32[512,128]{1,0:T(8,128)S(1)} custom-call(f32[512,128]{1,0:T(8,128)} %bitcast.3, f32[23]{0:T(128)} %fields_hbm.1, s32[4,6]{1,0:T(4,128)} %order_hbm.1), custom_call_target="tpu_custom_call" | custom-call | tf_op jit(solution)/shard_map/pallas_call | solution.py:394
  57.6 0.7 %copy.5 = f32[1,1,65536]{2,1,0:T(1,128)} copy(f32[1,1,65536]{2,1,0:T(1,128)S(1)} %bitcast.2) | data formatting | bytes 524288

commit v4 on v3

--- a/solution.py
+++ b/solution.py
@@ -140,6 +140,12 @@
             def _():
                 greet(at(z, i))
 
+        @pl.loop(z + 1, n_z)
+        def _(tz):
+            greet(at(tz, mine))
+
+        greet(at(0, 0))
+
     lane = lax.broadcasted_iota(jnp.int32, (1, 128), 1)
     row = lax.broadcasted_iota(jnp.int32, (128, 128), 0)
     col = lax.broadcasted_iota(jnp.int32, (128, 128), 1)
@@ -169,29 +175,43 @@
     @pl.when(me > 0)
     def _():
         whole = jnp.where(z > 0, plane - 1, plane - 2)
-        pl.semaphore_wait(barrier, whole + z)
-
-        @pl.loop(0, z)
-        def _(tz):
-            @pl.when(tz * plane + mine > 0)
+        column = jnp.where((z > 0) & (mine == 0), z - 1, z)
+        pl.semaphore_wait(barrier, whole + column)
+
+        @pl.loop(0, n_z - 1)
+        def _(t):
+            tz = far_first(t)
+
+            @pl.when((tz < z) & (tz * plane + mine > 0))
             def _():
                 pl.semaphore_signal(
                     ready.at[z], inc=1, device_id=at(tz, mine), device_id_type=MESH
                 )
 
-        @pl.loop(z + 1, n_z)
-        def _(tz):
-            greet(at(tz, mine))
-
-        @pl.when(mine == 1)
-        def _():
-            greet(at(0, 0))
-
-            @pl.when(z == 0)
+    @pl.when(z > 0)
+    def _():
+        for i in range(plane):
+
+            @pl.when(mine != i)
             def _():
-                @pl.loop(1, n_z)
-                def _(tz):
-                    greet(at(tz, 0))
+                pl.semaphore_signal(
+                    ready.at[n_z + 1], inc=1, device_id=at(z, i), device_id_type=MESH
+                )
+
+    @pl.when(me == 0)
+    def _():
+        pl.semaphore_wait(barrier, n - 1)
+
+        @pl.loop(0, n_z)
+        def _(t):
+            tz = far_first(t)
+            for i in range(plane):
+
+                @pl.when(tz * plane + i > 0)
+                def _():
+                    pl.semaphore_signal(
+                        ready.at[n_z], inc=1, device_id=at(tz, i), device_id_type=MESH
+                    )
 
     fetch.wait()
     for b in range(4):
@@ -242,20 +262,9 @@
         copy = pltpu.make_async_copy(source.at[part], target.at[part], send_sems.at[which])
         copy.wait()
 
-    @pl.when(me == 0)
-    def _():
-        pl.semaphore_wait(barrier, n_z)
-
-        @pl.loop(0, n_z)
-        def _(t):
-            tz = far_first(t)
-            for i in range(plane):
-
-                @pl.when(tz * plane + i > 0)
-                def _():
-                    pl.semaphore_signal(
-                        ready.at[n_z], inc=1, device_id=at(tz, i), device_id_type=MESH
-                    )
+    @pl.when(z > 0)
+    def _():
+        pl.semaphore_wait(ready.at[n_z + 1], plane - 1)
 
     @pl.loop(0, n_z - 1)
     def _(t):
@@ -414,7 +423,7 @@
             pltpu.SemaphoreType.DMA((1,)),
             pltpu.SemaphoreType.DMA((1,)),
             pltpu.SemaphoreType.DMA((3,)),
-            pltpu.SemaphoreType.REGULAR((n_z + 1,)),
+            pltpu.SemaphoreType.REGULAR((n_z + 2,)),
         ],
         compiler_params=pltpu.CompilerParams(
             collective_id=0, has_side_effects=True, vmem_limit_bytes=4 * 2**20

time: 58.4 us -> 58.3 us (level)
  no operation moved by 1% of the time
where the time goes in v4:
time: 58.3 us; the launch traced here: 58.2 us
  Pallas kernels  57.5 us (99%)
  local copies, waits for them, and re-layouts  0.71 us (1%)
    pallas_call x1, Pallas kernels, local(): pl.pallas_call(kernel, out_shape=jax.ShapeDtypeStruct((amps // 128, 128),...  57.5 us

profile of v4, /device:TPU:33, one launch (start us, length us, event | category | flops | bytes accessed | tf_op | source)
XLA Modules:
  0.0 58.2 jit_solution(9348637733446943558)
XLA Ops:
  0.0 57.5 %shard_map.37 = f32[512,128]{1,0:T(8,128)S(1)} custom-call(f32[512,128]{1,0:T(8,128)} %bitcast.3, f32[23]{0:T(128)} %fields_hbm.1, s32[4,6]{1,0:T(4,128)} %order_hbm.1), custom_call_target="tpu_custom_call" | custom-call | tf_op jit(solution)/shard_map/pallas_call | solution.py:403
  57.5 0.7 %copy.5 = f32[1,1,65536]{2,1,0:T(1,128)} copy(f32[1,1,65536]{2,1,0:T(1,128)S(1)} %bitcast.2) | data formatting | bytes 524288

commit v5 on v4

--- a/solution.py
+++ b/solution.py
@@ -140,11 +140,12 @@
             def _():
                 greet(at(z, i))
 
+        greet(at(0, 0))
+
         @pl.loop(z + 1, n_z)
         def _(tz):
-            greet(at(tz, mine))
-
-        greet(at(0, 0))
+            for i in range(plane):
+                greet(at(tz, i))
 
     lane = lax.broadcasted_iota(jnp.int32, (1, 128), 1)
     row = lax.broadcasted_iota(jnp.int32, (128, 128), 0)
@@ -174,9 +175,7 @@
 
     @pl.when(me > 0)
     def _():
-        whole = jnp.where(z > 0, plane - 1, plane - 2)
-        column = jnp.where((z > 0) & (mine == 0), z - 1, z)
-        pl.semaphore_wait(barrier, whole + column)
+        pl.semaphore_wait(barrier, jnp.where(z > 0, (z + 1) * plane - 2, plane - 2))
 
         @pl.loop(0, n_z - 1)
         def _(t):
@@ -187,31 +186,6 @@
                 pl.semaphore_signal(
                     ready.at[z], inc=1, device_id=at(tz, mine), device_id_type=MESH
                 )
-
-    @pl.when(z > 0)
-    def _():
-        for i in range(plane):
-
-            @pl.when(mine != i)
-            def _():
-                pl.semaphore_signal(
-                    ready.at[n_z + 1], inc=1, device_id=at(z, i), device_id_type=MESH
-                )
-
-    @pl.when(me == 0)
-    def _():
-        pl.semaphore_wait(barrier, n - 1)
-
-        @pl.loop(0, n_z)
-        def _(t):
-            tz = far_first(t)
-            for i in range(plane):
-
-                @pl.when(tz * plane + i > 0)
-                def _():
-                    pl.semaphore_signal(
-                        ready.at[n_z], inc=1, device_id=at(tz, i), device_id_type=MESH
-                    )
 
     fetch.wait()
     for b in range(4):
@@ -262,17 +236,31 @@
         copy = pltpu.make_async_copy(source.at[part], target.at[part], send_sems.at[which])
         copy.wait()
 
-    @pl.when(z > 0)
+    @pl.when(me == 0)
     def _():
-        pl.semaphore_wait(ready.at[n_z + 1], plane - 1)
+        pl.semaphore_wait(barrier, n - 1)
 
     @pl.loop(0, n_z - 1)
     def _(t):
         tz = far_first(t)
 
-        @pl.when((tz < z) | (me == 0))
+        @pl.when((tz < z) & (me > 0))
         def _():
             post_known(tz)
+
+        @pl.when(me == 0)
+        def _():
+            for i in range(plane):
+                pl.semaphore_signal(
+                    ready.at[n_z], inc=1, device_id=at(tz, i), device_id_type=MESH
+                )
+            for i in range(plane):
+                post(send, held, 0, tz, i)
+
+    @pl.when(me == 0)
+    def _():
+        for i in range(1, plane):
+            pl.semaphore_signal(ready.at[n_z], inc=1, device_id=at(z, i), device_id_type=MESH)
 
     for i in range(plane):
 
@@ -423,7 +411,7 @@
             pltpu.SemaphoreType.DMA((1,)),
             pltpu.SemaphoreType.DMA((1,)),
             pltpu.SemaphoreType.DMA((3,)),
-            pltpu.SemaphoreType.REGULAR((n_z + 2,)),
+            pltpu.SemaphoreType.REGULAR((n_z + 1,)),
         ],
         compiler_params=pltpu.CompilerParams(
             collective_id=0, has_side_effects=True, vmem_limit_bytes=4 * 2**20

time: 58.3 us -> 58 us (level)
  no operation moved by 1% of the time
where the time goes in v5:
time: 58 us; the launch traced here: 57.9 us
  Pallas kernels  57.2 us (99%)
  local copies, waits for them, and re-layouts  0.71 us (1%)
    pallas_call x1, Pallas kernels, local(): pl.pallas_call(kernel, out_shape=jax.ShapeDtypeStruct((amps // 128, 128),...  57.2 us

profile of v5, /device:TPU:33, one launch (start us, length us, event | category | flops | bytes accessed | tf_op | source)
XLA Modules:
  0.0 57.9 jit_solution(17650824612306523457)
XLA Ops:
  0.0 57.2 %shard_map.37 = f32[512,128]{1,0:T(8,128)S(1)} custom-call(f32[512,128]{1,0:T(8,128)} %bitcast.3, f32[23]{0:T(128)} %fields_hbm.1, s32[4,6]{1,0:T(4,128)} %order_hbm.1), custom_call_target="tpu_custom_call" | custom-call | tf_op jit(solution)/shard_map/pallas_call | solution.py:391
  57.2 0.7 %copy.5 = f32[1,1,65536]{2,1,0:T(1,128)} copy(f32[1,1,65536]{2,1,0:T(1,128)S(1)} %bitcast.2) | data formatting | bytes 524288

commit v6 on v5

--- a/solution.py
+++ b/solution.py
@@ -12,6 +12,7 @@
 BOOST = 1.161834242728283
 EPSILON = 1e-06
 STARTS = (0, 7, 9, 1)
+IDLE = 1
 
 
 def gate_entries(left, right, shape):
@@ -127,12 +128,22 @@
         dz = n_z // 2 + ((t + 1) // 2) * (2 * (t % 2) - 1)
         return (z + dz + n_z) % n_z
 
+    busy = n_z - IDLE
+    hosting = (z < busy) & (me > 0)
+    extra_row = (z < IDLE) & (me > 0)
+    extra_zero = (mine == 0) & (z == IDLE)
+    extra_last = (mine == 0) & (z == IDLE + 1)
+    double = extra_row | extra_zero | extra_last
+    hosted = jnp.where(hosting, jnp.where(double, 2, 1), 0)
+    second = jnp.where(
+        extra_row, me + busy * plane, jnp.where(extra_last, busy * plane, 0)
+    )
     barrier = pltpu.get_barrier_semaphore()
 
     def greet(device):
         pl.semaphore_signal(barrier, inc=1, device_id=device, device_id_type=MESH)
 
-    @pl.when(me > 0)
+    @pl.when(hosting)
     def _():
         for i in range(plane):
 
@@ -147,6 +158,8 @@
             for i in range(plane):
                 greet(at(tz, i))
 
+    got_z[...] = jnp.zeros_like(got_z)
+    part_z[...] = jnp.zeros_like(part_z)
     lane = lax.broadcasted_iota(jnp.int32, (1, 128), 1)
     row = lax.broadcasted_iota(jnp.int32, (128, 128), 0)
     col = lax.broadcasted_iota(jnp.int32, (128, 128), 1)
@@ -173,7 +186,7 @@
         for m in w3t
     ]
 
-    @pl.when(me > 0)
+    @pl.when(hosting)
     def _():
         pl.semaphore_wait(barrier, jnp.where(z > 0, (z + 1) * plane - 2, plane - 2))
 
@@ -186,6 +199,10 @@
                 pl.semaphore_signal(
                     ready.at[z], inc=1, device_id=at(tz, mine), device_id_type=MESH
                 )
+
+    @pl.when(jnp.logical_not(hosting))
+    def _():
+        pl.semaphore_wait(barrier, busy * plane - 1)
 
     fetch.wait()
     for b in range(4):
@@ -204,81 +221,98 @@
                     64 * n15 : 64 * (n15 + 1), 128 * n7 : 128 * (n7 + 1)
                 ]
 
-    def post(source, target, which, tz, i):
-        source, target = source.reshape(n, 4, 128), target.reshape(n, 4, 128)
+    def post(source, from_row, target, to_row, which, arrival, device):
         pltpu.make_async_remote_copy(
-            src_ref=source.at[tz * plane + i],
-            dst_ref=target.at[me],
+            src_ref=source.at[from_row],
+            dst_ref=target.at[to_row],
             send_sem=send_sems.at[which],
-            recv_sem=recv_sems.at[which],
-            device_id=at(tz, i),
+            recv_sem=recv_sems.at[arrival],
+            device_id=device,
             device_id_type=MESH,
         ).start()
 
-    def keep(source, target):
-        source, target = source.reshape(n, 4, 128), target.reshape(n, 4, 128)
-        target[me] = source[me]
-
-    def post_known(tz):
-        for i in range(plane):
-            if i == 0:
-                pl.when(tz > 0)(functools.partial(post, send, held, 0, tz, i))
-            else:
-                post(send, held, 0, tz, i)
-
-    def arrived(source, target, which):
-        part = pl.ds(0, 4 * (n - 1))
-        copy = pltpu.make_async_copy(source.at[part], target.at[part], recv_sems.at[which])
-        copy.wait()
-
-    def sent(source, target, which):
-        part = pl.ds(0, 4 * (n - 1))
-        copy = pltpu.make_async_copy(source.at[part], target.at[part], send_sems.at[which])
-        copy.wait()
-
-    @pl.when(me == 0)
-    def _():
-        pl.semaphore_wait(barrier, n - 1)
+    blocks = send.reshape(n, 4, 128)
+    held_blocks = held.reshape(2 * n, 4, 128)
+    back_blocks = back.reshape(2 * n, 4, 128)
+    final_blocks = final.reshape(n, 4, 128)
+
+    def give(row, slot, tz, i):
+        post(blocks, row, held_blocks, slot * n + me, 0, slot, at(tz, i))
+
+    def give_plane(tz):
+        @pl.when(tz > 0)
+        def _():
+            give(tz * plane, 0, tz, 0)
+
+        for i in range(1, plane):
+            give(tz * plane + i, 0, tz, i)
+
+        @pl.when(tz < IDLE)
+        def _():
+            if IDLE > 1:
+
+                @pl.when(tz > 0)
+                def _():
+                    give((tz + busy) * plane, 1, tz, 0)
+
+            for i in range(1, plane):
+                give((tz + busy) * plane + i, 1, tz, i)
+
+        @pl.when(tz == IDLE)
+        def _():
+            give(0, 1, tz, 0)
+
+        @pl.when(tz == IDLE + 1)
+        def _():
+            give(busy * plane, 1, tz, 0)
+
+    def await_blocks(semaphore, count):
+        blocks_of = held_blocks.at[pl.ds(0, count)]
+        pltpu.make_async_copy(blocks_of, blocks_of, semaphore).wait()
 
     @pl.loop(0, n_z - 1)
     def _(t):
         tz = far_first(t)
 
-        @pl.when((tz < z) & (me > 0))
-        def _():
-            post_known(tz)
-
-        @pl.when(me == 0)
-        def _():
-            for i in range(plane):
-                pl.semaphore_signal(
-                    ready.at[n_z], inc=1, device_id=at(tz, i), device_id_type=MESH
-                )
-            for i in range(plane):
-                post(send, held, 0, tz, i)
-
-    @pl.when(me == 0)
-    def _():
-        for i in range(1, plane):
-            pl.semaphore_signal(ready.at[n_z], inc=1, device_id=at(z, i), device_id_type=MESH)
-
-    for i in range(plane):
-
-        @pl.when((i != mine) & (z * plane + i > 0))
-        def _():
-            post(send, held, 0, z, i)
+        @pl.when((tz < busy) & ((tz < z) | (me == 0)))
+        def _():
+            give_plane(tz)
+
+    @pl.when(z < busy)
+    def _():
+        for i in range(plane):
+
+            @pl.when((i != mine) & (z * plane + i > 0))
+            def _():
+                give(z * plane + i, 0, z, i)
+
+                @pl.when(z < IDLE)
+                def _():
+                    give((z + busy) * plane + i, 1, z, i)
+
+        @pl.when((mine > 0) & (z == IDLE))
+        def _():
+            give(0, 1, z, 0)
+
+        @pl.when((mine > 0) & (z == IDLE + 1))
+        def _():
+            give(busy * plane, 1, z, 0)
 
     @pl.when(me > 0)
     def _():
-        @pl.loop(z + 1, n_z)
+        @pl.loop(z + 1, busy)
         def _(tz):
             pl.semaphore_wait(ready.at[tz], 1)
-            post_known(tz)
-
-        pl.semaphore_wait(ready.at[n_z], 1)
-        post(send, held, 0, 0, 0)
-
-    keep(send, held)
+            give_plane(tz)
+
+    @pl.when(hosting)
+    def _():
+        held_blocks[me] = blocks[me]
+
+    @pl.when(double)
+    def _():
+        held_blocks[n + me] = blocks[second]
+
     entries = [
         gate_entries(fields[15 + k], fields[16 + k], (1, 128)) for k in range(7)
     ]
@@ -294,29 +328,31 @@
     f16_0 = jnp.where(bit2 == 0, 0.0, flip)
     d16_1 = jnp.where(bit2 == 0, up, high)
     f16_1 = jnp.where(bit2 == 0, flip, 0.0)
-    arrived(send, held, 0)
-
-    for c in range(n // 8):
-        v = held[32 * c : 32 * (c + 1), :].reshape(4, 8, 128)
-        v = v * d15 + pltpu.roll(v, 2, 1) * below15 + pltpu.roll(v, 6, 1) * above15
-        v = v.reshape(2, 2, 8, 128)
-        v0, v1 = v[:, 0], v[:, 1]
-        u0 = v0 * d16_0 + pltpu.roll(v1, 4, 1) * f16_0
-        u1 = v1 * d16_1 + pltpu.roll(v0, 4, 1) * f16_1
-        v = jnp.stack([u0, u1], axis=1).reshape(32, 128)
-        t_ref[32 * c : 32 * (c + 1), :] = mix(v, entries[2], 3)
-    total = jnp.zeros((8, 128), jnp.float32)
-    for h in range(2):
-        v = jnp.concatenate(
-            [t_ref[16 * g + 8 * h : 16 * g + 8 * h + 8, :] for g in range(4 * n // 16)], axis=0
-        )
-        for k in range(4):
-            v = mix(v, entries[3 + k], 3 + k)
-        total = total + jnp.sum((v * v).reshape(-1, 8, 128), axis=0)
-        for g in range(4 * n // 16):
-            back[16 * g + 8 * h : 16 * g + 8 * h + 8, :] = v[8 * g : 8 * (g + 1)]
-
-    part_z[...] = jnp.sum(total, axis=0, keepdims=True)
+    @pl.loop(0, hosted)
+    def _(slot):
+        await_blocks(recv_sems.at[slot], n - 1)
+        for c in range(n // 8):
+            v = held[pl.ds(pl.multiple_of(4 * n * slot + 32 * c, 32), 32), :].reshape(4, 8, 128)
+            v = v * d15 + pltpu.roll(v, 2, 1) * below15 + pltpu.roll(v, 6, 1) * above15
+            v = v.reshape(2, 2, 8, 128)
+            v0, v1 = v[:, 0], v[:, 1]
+            u0 = v0 * d16_0 + pltpu.roll(v1, 4, 1) * f16_0
+            u1 = v1 * d16_1 + pltpu.roll(v0, 4, 1) * f16_1
+            v = jnp.stack([u0, u1], axis=1).reshape(32, 128)
+            t_ref[32 * c : 32 * (c + 1), :] = mix(v, entries[2], 3)
+        total = jnp.zeros((8, 128), jnp.float32)
+        for h in range(2):
+            v = jnp.concatenate(
+                [t_ref[16 * g + 8 * h : 16 * g + 8 * h + 8, :] for g in range(4 * n // 16)],
+                axis=0,
+            )
+            for k in range(4):
+                v = mix(v, entries[3 + k], 3 + k)
+            total = total + jnp.sum((v * v).reshape(-1, 8, 128), axis=0)
+            for g in range(4 * n // 16):
+                rows = pl.ds(pl.multiple_of(4 * n * slot + 16 * g + 8 * h, 8), 8)
+                back[rows, :] = v[8 * g : 8 * (g + 1)]
+        part_z[...] += jnp.sum(total, axis=0, keepdims=True)
 
     def small(source, target, slot, px, py, s_sem, r_sem):
         return pltpu.make_async_remote_copy(
@@ -328,29 +364,56 @@
             device_id_type=MESH,
         )
 
-    @pl.loop(1, n_z)
-    def _(k):
-        tz = (z + k) % n_z
-        small(part_z, got_z, z, 2 * tz + core, gy, send_sems.at[2], got_z_sem.at[0]).start()
-
-    got_z[z] = part_z[...]
-
-    @pl.loop(0, n_z - 1)
-    def _(t):
-        tz = far_first(t)
+    @pl.when(hosting)
+    def _():
+        @pl.loop(1, n_z)
+        def _(k):
+            tz = (z + k) % n_z
+            small(part_z, got_z, z, 2 * tz + core, gy, send_sems.at[2], got_z_sem.at[0]).start()
+
+        got_z[z] = part_z[...]
+
+    def give_back(slot, row, tz, i):
+        post(back_blocks, slot * n + tz * plane + i, final_blocks, row, 1, 2, at(tz, i))
+
+    @pl.when(hosting)
+    def _():
+        @pl.loop(0, n_z - 1)
+        def _(t):
+            tz = far_first(t)
+            for i in range(plane):
+                give_back(0, me, tz, i)
+
+            @pl.when(double)
+            def _():
+                for i in range(plane):
+                    give_back(1, second, tz, i)
+
         for i in range(plane):
-            post(back, final, 1, tz, i)
-
-    for i in range(plane):
-
-        @pl.when(i != mine)
-        def _():
-            post(back, final, 1, z, i)
-
-    keep(back, final)
-    pltpu.make_async_copy(
-        got_z.at[pl.ds(0, n_z - 1)], got_z.at[pl.ds(0, n_z - 1)], got_z_sem.at[0]
-    ).wait()
+
+            @pl.when(i != mine)
+            def _():
+                give_back(0, me, z, i)
+
+                @pl.when(double)
+                def _():
+                    give_back(1, second, z, i)
+
+        final_blocks[me] = back_blocks[me]
+
+    @pl.when(double)
+    def _():
+        final_blocks[second] = back_blocks[n + me]
+
+    def await_small(target, semaphore, count):
+        rows = target.at[pl.ds(0, count)]
+        pltpu.make_async_copy(rows, rows, semaphore).wait()
+
+    others = busy - jnp.where(hosting, 1, 0) - jnp.where(mine == 0, 1, 0)
+    for count in range(busy - 2, busy + 1):
+        pl.when(others == count)(
+            functools.partial(await_small, got_z, got_z_sem.at[0], count)
+        )
     part_xc[...] = jnp.sum(got_z[...], axis=0)
 
     @pl.loop(1, 2 * n_x)
@@ -359,26 +422,29 @@
         small(part_xc, got_xc, mine, 2 * z + tc, tx, send_sems.at[3], got_xc_sem.at[0]).start()
 
     got_xc[mine] = part_xc[...]
-    pltpu.make_async_copy(
-        got_xc.at[pl.ds(0, 2 * n_x - 1)], got_xc.at[pl.ds(0, 2 * n_x - 1)], got_xc_sem.at[0]
-    ).wait()
+    await_small(got_xc, got_xc_sem.at[0], plane - 1)
     summed = jnp.sum(jnp.sum(got_xc[...], axis=0), axis=1, keepdims=True)
     count = float(x_ref.shape[0] * x_ref.shape[1] * n)
     scale = lax.rsqrt(summed / count + EPSILON)
-    arrived(back, final, 1)
+    for count in range(3):
+        pl.when(hosted == count)(
+            functools.partial(await_blocks, recv_sems.at[2], n - count)
+        )
     for n15 in range(2):
         for n7 in range(2):
             o_ref[pl.ds(n15 * 256 + n7, 128, stride=2), :] = (
                 final[pl.ds(2 * n15 + n7, 128, stride=4), :] * scale
             )
-    sent(send, held, 0)
-    sent(back, final, 1)
-    pltpu.make_async_copy(
-        got_z.at[pl.ds(0, n_z - 1)], got_z.at[pl.ds(0, n_z - 1)], send_sems.at[2]
-    ).wait()
-    pltpu.make_async_copy(
-        got_xc.at[pl.ds(0, 2 * n_x - 1)], got_xc.at[pl.ds(0, 2 * n_x - 1)], send_sems.at[3]
-    ).wait()
+    for count in range(3):
+
+        @pl.when(hosted == count)
+        def _():
+            await_blocks(send_sems.at[0], n - count)
+            if count > 0:
+                await_blocks(send_sems.at[1], count * (n - 1))
+                await_small(got_z, send_sems.at[2], n_z - 1)
+
+    await_small(got_xc, send_sems.at[3], plane - 1)
 
 
 def local(initial_state, fields, bond_order):
@@ -386,6 +452,7 @@
     n = lax.axis_size("gx") * lax.axis_size("gy")
     n_z, n_xc = lax.axis_size("gx") // 2, 2 * lax.axis_size("gy")
     block = pltpu.VMEM((amps // 128, 128), jnp.float32)
+    slots = pltpu.VMEM((2 * amps // 128, 128), jnp.float32)
     vmem, hbm = pl.BlockSpec(memory_space=pltpu.VMEM), pl.BlockSpec(memory_space=pltpu.HBM)
     pin = functools.partial(pltpu.with_memory_space_constraint, memory_space=pltpu.HBM)
     out = pl.pallas_call(
@@ -399,19 +466,19 @@
             block,
             block,
             block,
-            block,
-            block,
+            slots,
+            slots,
             block,
             pltpu.VMEM((1, 128), jnp.float32),
             pltpu.VMEM((1, 128), jnp.float32),
             pltpu.VMEM((n_z, 1, 128), jnp.float32),
             pltpu.VMEM((n_xc, 1, 128), jnp.float32),
             pltpu.SemaphoreType.DMA((4,)),
-            pltpu.SemaphoreType.DMA((2,)),
+            pltpu.SemaphoreType.DMA((3,)),
             pltpu.SemaphoreType.DMA((1,)),
             pltpu.SemaphoreType.DMA((1,)),
             pltpu.SemaphoreType.DMA((3,)),
-            pltpu.SemaphoreType.REGULAR((n_z + 1,)),
+            pltpu.SemaphoreType.REGULAR((n_z,)),
         ],
         compiler_params=pltpu.CompilerParams(
             collective_id=0, has_side_effects=True, vmem_limit_bytes=4 * 2**20

time: 58 us -> 60.1 us (1.036)
  Pallas kernels: 57.2 us -> 59.3 us
    pallas_call x1, Pallas kernels: 57.2 us -> 59.3 us  [local(): pl.pallas_call(kernel, out_shape=jax.ShapeDtypeStruct((amps // 128, 128),...]
where the time goes in v6:
time: 60.1 us; the launch traced here: 60 us
  Pallas kernels  59.3 us (99%)
  local copies, waits for them, and re-layouts  0.71 us (1%)
    pallas_call x1, Pallas kernels, local(): pl.pallas_call(kernel, out_shape=jax.ShapeDtypeStruct((amps // 128, 128),...  59.3 us

profile of v6, /device:TPU:33, one launch (start us, length us, event | category | flops | bytes accessed | tf_op | source)
XLA Modules:
  0.0 60.0 jit_solution(1526411516089608553)
XLA Ops:
  0.0 59.3 %shard_map.37 = f32[512,128]{1,0:T(8,128)S(1)} custom-call(f32[512,128]{1,0:T(8,128)} %bitcast.3, f32[23]{0:T(128)} %fields_hbm.1, s32[4,6]{1,0:T(4,128)} %order_hbm.1), custom_call_target="tpu_custom_call" | custom-call | tf_op jit(solution)/shard_map/pallas_call | solution.py:458
  59.3 0.7 %copy.5 = f32[1,1,65536]{2,1,0:T(1,128)} copy(f32[1,1,65536]{2,1,0:T(1,128)S(1)} %bitcast.2) | data formatting | bytes 524288

commit v7 on v5

--- a/solution.py
+++ b/solution.py
@@ -147,6 +147,20 @@
             for i in range(plane):
                 greet(at(tz, i))
 
+    @pl.when(me > 0)
+    def _():
+        pl.semaphore_wait(barrier, jnp.where(z > 0, (z + 1) * plane - 2, plane - 2))
+
+        @pl.loop(0, n_z - 1)
+        def _(t):
+            tz = far_first(t)
+
+            @pl.when((tz < z) & (tz * plane + mine > 0))
+            def _():
+                pl.semaphore_signal(
+                    ready.at[z], inc=1, device_id=at(tz, mine), device_id_type=MESH
+                )
+
     lane = lax.broadcasted_iota(jnp.int32, (1, 128), 1)
     row = lax.broadcasted_iota(jnp.int32, (128, 128), 0)
     col = lax.broadcasted_iota(jnp.int32, (128, 128), 1)
@@ -173,20 +187,6 @@
         for m in w3t
     ]
 
-    @pl.when(me > 0)
-    def _():
-        pl.semaphore_wait(barrier, jnp.where(z > 0, (z + 1) * plane - 2, plane - 2))
-
-        @pl.loop(0, n_z - 1)
-        def _(t):
-            tz = far_first(t)
-
-            @pl.when((tz < z) & (tz * plane + mine > 0))
-            def _():
-                pl.semaphore_signal(
-                    ready.at[z], inc=1, device_id=at(tz, mine), device_id_type=MESH
-                )
-
     fetch.wait()
     for b in range(4):
         rows = slice(128 * b, 128 * (b + 1))
@@ -240,27 +240,25 @@
     def _():
         pl.semaphore_wait(barrier, n - 1)
 
+        def ready_plane(tz, first):
+            for i in range(first, plane):
+                pl.semaphore_signal(
+                    ready.at[n_z], inc=1, device_id=at(tz, i), device_id_type=MESH
+                )
+
+        @pl.loop(0, n_z - 1)
+        def _(t):
+            ready_plane(far_first(t), 0)
+
+        ready_plane(z, 1)
+
     @pl.loop(0, n_z - 1)
     def _(t):
         tz = far_first(t)
 
-        @pl.when((tz < z) & (me > 0))
+        @pl.when((tz < z) | (me == 0))
         def _():
             post_known(tz)
-
-        @pl.when(me == 0)
-        def _():
-            for i in range(plane):
-                pl.semaphore_signal(
-                    ready.at[n_z], inc=1, device_id=at(tz, i), device_id_type=MESH
-                )
-            for i in range(plane):
-                post(send, held, 0, tz, i)
-
-    @pl.when(me == 0)
-    def _():
-        for i in range(1, plane):
-            pl.semaphore_signal(ready.at[n_z], inc=1, device_id=at(z, i), device_id_type=MESH)
 
     for i in range(plane):
 

time: 58 us -> 58.4 us (level)
  no operation moved by 1% of the time
where the time goes in v7:
time: 58.4 us; the launch traced here: 58.2 us
  Pallas kernels  57.5 us (98%)
  local copies, waits for them, and re-layouts  0.71 us (1%)
    pallas_call x1, Pallas kernels, local(): pl.pallas_call(kernel, out_shape=jax.ShapeDtypeStruct((amps // 128, 128),...  57.5 us

profile of v7, /device:TPU:33, one launch (start us, length us, event | category | flops | bytes accessed | tf_op | source)
XLA Modules:
  0.0 58.2 jit_solution(6214980725812059183)
XLA Ops:
  0.0 57.5 %shard_map.37 = f32[512,128]{1,0:T(8,128)S(1)} custom-call(f32[512,128]{1,0:T(8,128)} %bitcast.3, f32[23]{0:T(128)} %fields_hbm.1, s32[4,6]{1,0:T(4,128)} %order_hbm.1), custom_call_target="tpu_custom_call" | custom-call | tf_op jit(solution)/shard_map/pallas_call | solution.py:389
  57.5 0.7 %copy.5 = f32[1,1,65536]{2,1,0:T(1,128)} copy(f32[1,1,65536]{2,1,0:T(1,128)S(1)} %bitcast.2) | data formatting | bytes 524288

commit v8 on v5

--- a/solution.py
+++ b/solution.py
@@ -173,20 +173,6 @@
         for m in w3t
     ]
 
-    @pl.when(me > 0)
-    def _():
-        pl.semaphore_wait(barrier, jnp.where(z > 0, (z + 1) * plane - 2, plane - 2))
-
-        @pl.loop(0, n_z - 1)
-        def _(t):
-            tz = far_first(t)
-
-            @pl.when((tz < z) & (tz * plane + mine > 0))
-            def _():
-                pl.semaphore_signal(
-                    ready.at[z], inc=1, device_id=at(tz, mine), device_id_type=MESH
-                )
-
     fetch.wait()
     for b in range(4):
         rows = slice(128 * b, 128 * (b + 1))
@@ -203,6 +189,20 @@
                 send[pl.ds(4 * n8 + 2 * n15 + n7, 64, stride=8), :] = out[
                     64 * n15 : 64 * (n15 + 1), 128 * n7 : 128 * (n7 + 1)
                 ]
+
+    @pl.when(me > 0)
+    def _():
+        pl.semaphore_wait(barrier, jnp.where(z > 0, (z + 1) * plane - 2, plane - 2))
+
+        @pl.loop(0, n_z - 1)
+        def _(t):
+            tz = far_first(t)
+
+            @pl.when((tz < z) & (tz * plane + mine > 0))
+            def _():
+                pl.semaphore_signal(
+                    ready.at[z], inc=1, device_id=at(tz, mine), device_id_type=MESH
+                )
 
     def post(source, target, which, tz, i):
         source, target = source.reshape(n, 4, 128), target.reshape(n, 4, 128)

time: 58 us -> 58.5 us (level)
  no operation moved by 1% of the time
where the time goes in v8:
time: 58.5 us; the launch traced here: 58.4 us
  Pallas kernels  57.7 us (99%)
  local copies, waits for them, and re-layouts  0.71 us (1%)
    pallas_call x1, Pallas kernels, local(): pl.pallas_call(kernel, out_shape=jax.ShapeDtypeStruct((amps // 128, 128),...  57.7 us

profile of v8, /device:TPU:33, one launch (start us, length us, event | category | flops | bytes accessed | tf_op | source)
XLA Modules:
  0.0 58.4 jit_solution(9825817314881013924)
XLA Ops:
  0.0 57.7 %shard_map.37 = f32[512,128]{1,0:T(8,128)S(1)} custom-call(f32[512,128]{1,0:T(8,128)} %bitcast.3, f32[23]{0:T(128)} %fields_hbm.1, s32[4,6]{1,0:T(4,128)} %order_hbm.1), custom_call_target="tpu_custom_call" | custom-call | tf_op jit(solution)/shard_map/pallas_call | solution.py:391
  57.7 0.7 %copy.5 = f32[1,1,65536]{2,1,0:T(1,128)} copy(f32[1,1,65536]{2,1,0:T(1,128)S(1)} %bitcast.2) | data formatting | bytes 524288

commit v9 on v5

--- a/solution.py
+++ b/solution.py
@@ -44,6 +44,12 @@
     from_below = jnp.where(equal, 0.0, jnp.where(zero, flip, 0.0))
     from_above = jnp.where(equal, 0.0, jnp.where(zero, 0.0, flip))
     shift = jnp.left_shift(1, offset)
+    if matrix is None:
+        row = lax.broadcasted_iota(jnp.int32, (128, 128), 0)
+        col = lax.broadcasted_iota(jnp.int32, (128, 128), 1)
+        moved = jnp.where(row == col - shift, from_below, 0.0)
+        moved = jnp.where(row == col + shift, from_above, moved)
+        return jnp.where(row == col, diagonal, moved)
     return (
         matrix * diagonal
         + pltpu.roll(matrix, shift, 1) * from_below
@@ -148,12 +154,9 @@
                 greet(at(tz, i))
 
     lane = lax.broadcasted_iota(jnp.int32, (1, 128), 1)
-    row = lax.broadcasted_iota(jnp.int32, (128, 128), 0)
-    col = lax.broadcasted_iota(jnp.int32, (128, 128), 1)
     fetch_fields.wait()
     fetch_order.wait()
-    identity = jnp.where(row == col, 1.0, 0.0)
-    mats = [identity] * 4
+    mats = [None] * 4
     for e in range(6):
         for w in range(4):
             step = e if w in (0, 3) else 5 - e

time: 58 us -> 58 us (level)
  no operation moved by 1% of the time
where the time goes in v9:
time: 58 us; the launch traced here: 57.9 us
  Pallas kernels  57.1 us (98%)
  local copies, waits for them, and re-layouts  0.71 us (1%)
    pallas_call x1, Pallas kernels, local(): pl.pallas_call(kernel, out_shape=jax.ShapeDtypeStruct((amps // 128, 128),...  57.1 us

profile of v9, /device:TPU:33, one launch (start us, length us, event | category | flops | bytes accessed | tf_op | source)
XLA Modules:
  0.0 57.9 jit_solution(11913165021918131986)
XLA Ops:
  0.0 57.1 %shard_map.37 = f32[512,128]{1,0:T(8,128)S(1)} custom-call(f32[512,128]{1,0:T(8,128)} %bitcast.3, f32[23]{0:T(128)} %fields_hbm.1, s32[4,6]{1,0:T(4,128)} %order_hbm.1), custom_call_target="tpu_custom_call" | custom-call | tf_op jit(solution)/shard_map/pallas_call | solution.py:394
  57.1 0.7 %copy.5 = f32[1,1,65536]{2,1,0:T(1,128)} copy(f32[1,1,65536]{2,1,0:T(1,128)S(1)} %bitcast.2) | data formatting | bytes 524288
